TPU v7x, 512 devices: a whole 4x8x8 slice. The times are simulated.
512 devices in a mesh: site: 32 (over x, z), clade: 16 (over y, core).
Axes of the slice: x: 4, y: 8, z: 8, core: 2. Of those that a mesh axis runs over, the one named last changes fastest.
Arguments:
- tips: int32 [512, 131072], P('clade', 'site'), may hold values from 0 to 4
- transition: float32 [992, 4, 4, 4], P('clade'), may hold values from 0 to 1, as said below
- clade_children: int32 [496, 2], P('clade'), may hold values from 0 to 61, as said below
- upper_transition: float32 [30, 4, 4, 4], replicated, may hold values from 0 to 1, as said below
- upper_children: int32 [15, 2], replicated, may hold values from 0 to 29, as said below
- pattern_weights: int32 [131072], P('site'), may hold values from 1 to 8
Outputs:
- weighted_loglik: float32 [131072], P(('site', 'clade'))
- mean_loglik: float32 [], replicated
Inputs may be any that keep to these rules, and one draw needn't show every extreme that they name: `tips`: code 4 marks a gap or an unknown base. `transition`: every row of every 4 x 4 block is positive and sums to 1. `upper_transition`: every row of every 4 x 4 block is positive and sums to 1. `clade_children`: rows k * (31) to (k + 1) * 31 - 1 belong to clade k; its row j holds two different node numbers below 32 + j, and each node 0 to 61 of the clade is a child in exactly one row of the clade. `upper_children`: row j holds two different node numbers below 16 + j, and each node 0 to 29 is a child in exactly one row.
All inputs are finite; a program needn't handle non-finite values.
Results may differ from a plain program's by a relative error of at most 0.0003.
Values sent between devices are 32-bit elements; how exact they have to be, the bound alone decides.
No kernel may reach another device: no remote copies, remote signals or barrier semaphores. Data moves between devices by JAX's collectives and lax.ppermute only.
A program may use at most 64 MiB of HBM per device.

v0:
```python
import functools

import jax
import jax.numpy as jnp
from jax import lax
from jax.sharding import Mesh
from jax.sharding import PartitionSpec as P

CLADE = ("clade_0", "clade_1")
SITE_CLADE = ("site_0", "site_1", "clade_0", "clade_1")
SITE = ("site_0", "site_1")


def cut_along(shard, dim, devices):
    before, after = (shard.shape[:dim], shard.shape[dim + 1 :])
    return jnp.moveaxis(shard.reshape(*before, devices, -1, *after), dim, 0)


def in_order(blocks, dim):
    lengths = list(blocks.shape[1:])
    lengths[dim] *= blocks.shape[0]
    return jnp.moveaxis(blocks, 0, dim).reshape(lengths)


def turned_blocks(blocks, axes, turns):
    lengths = [lax.axis_size(a) for a in axes]
    blocks = blocks.reshape(*lengths, *blocks.shape[1:])
    for k in turns:
        blocks = lax.all_to_all(blocks, axes[k], split_axis=k, concat_axis=k, tiled=True)
    return blocks.reshape(-1, *blocks.shape[len(axes) :])


def exchange_by_chip(shard, groups, turns, split_dim, concat_dim):
    devices = lax.axis_size(groups[0]) * lax.axis_size(groups[1])
    blocks = cut_along(shard, split_dim, devices)
    return in_order(turned_blocks(blocks, groups, turns), concat_dim)


def by_axis(shard, axes):
    return functools.reduce(lax.psum, axes, shard)


def transform(matrix, values_in):
    total = matrix[:, :, 0, None] * values_in[:, 0, None, :]
    for state in range(1, 4):
        total = total + matrix[:, :, state, None] * values_in[:, state, None, :]
    return total


def prune_tree(partials, scales, matrices, merges, first_new):

    def advance(node_index, state_pair):
        cur_parts, cur_scales = state_pair
        left_index = merges[node_index, 0]
        right_index = merges[node_index, 1]
        left_part = lax.dynamic_index_in_dim(cur_parts, left_index, 0, keepdims=False)
        right_part = lax.dynamic_index_in_dim(cur_parts, right_index, 0, keepdims=False)
        left_branch = lax.dynamic_index_in_dim(matrices, left_index, 0, keepdims=False)
        right_branch = lax.dynamic_index_in_dim(matrices, right_index, 0, keepdims=False)
        left_scale = lax.dynamic_index_in_dim(cur_scales, left_index, 0, keepdims=False)
        right_scale = lax.dynamic_index_in_dim(cur_scales, right_index, 0, keepdims=False)
        product = transform(left_branch, left_part) * transform(right_branch, right_part)
        biggest = jnp.max(product, axis=(0, 1))
        new_scale = left_scale + right_scale + jnp.log(biggest)
        target = (first_new + node_index).astype(jnp.int32)
        cur_parts = lax.dynamic_update_index_in_dim(cur_parts, product / biggest, target, 0)
        cur_scales = lax.dynamic_update_index_in_dim(cur_scales, new_scale, target, 0)
        return (cur_parts, cur_scales)

    return lax.fori_loop(0, merges.shape[0], advance, (partials, scales))


def tip_partials(tip_codes, rate_count):
    states = jnp.arange(4, dtype=jnp.int32)
    matches = (tip_codes[:, None, :] == states[None, :, None]) | (tip_codes[:, None, :] == 4)
    single = matches.astype(jnp.float32)
    return jnp.broadcast_to(single[:, None], (single.shape[0], rate_count, 4, single.shape[2]))


def clade_root(tip_codes, matrices, merges):
    leaf_count = tip_codes.shape[0]
    site_count = tip_codes.shape[1]
    rate_count = matrices.shape[1]
    leaves = tip_partials(tip_codes, rate_count)
    partials = jnp.concatenate(
        [leaves, jnp.zeros((leaf_count - 1, rate_count, 4, site_count), jnp.float32)], axis=0
    )
    scales = jnp.zeros((2 * leaf_count - 1, site_count), jnp.float32)
    partials, scales = prune_tree(partials, scales, matrices, merges, leaf_count)
    return (partials[-1], scales[-1])


def upper_root(root_parts, root_scales, matrices, merges):
    clade_total = root_parts.shape[0]
    partials = jnp.concatenate(
        [root_parts, jnp.zeros((clade_total - 1,) + root_parts.shape[1:], jnp.float32)], axis=0
    )
    scales = jnp.concatenate(
        [root_scales, jnp.zeros((clade_total - 1, root_scales.shape[1]), jnp.float32)], axis=0
    )
    partials, scales = prune_tree(partials, scales, matrices, merges, clade_total)
    return (partials[-1], scales[-1])


def site_loglik(root_part, root_scale, weights, taxa_total):
    summed = jnp.sum(root_part, axis=(0, 1)) / (4.0 * root_part.shape[0])
    return weights.astype(jnp.float32) * (jnp.log(summed) + root_scale) / taxa_total


def per_device(tips, transition, clade_children, upper_transition, upper_children, pattern_weights):
    leaf_count = tips.shape[0]
    site_count = tips.shape[1]
    clades = lax.axis_size(CLADE)
    position = lax.axis_index(CLADE)
    piece_len = site_count // clades
    taxa_total = float(leaf_count * clades)
    root_part, root_scale = clade_root(tips, transition, clade_children)
    own_weights = lax.dynamic_slice_in_dim(pattern_weights, position * piece_len, piece_len, 0)
    scale_block = root_scale.reshape((1, 1, 1, site_count))
    every_part, every_scale = (
        exchange_by_chip(root_part[None], ("clade_0", "clade_1"), (0, 1), 3, 0),
        exchange_by_chip(scale_block, ("clade_0", "clade_1"), (0, 1), 3, 0),
    )
    every_scale = every_scale.reshape((clades, piece_len))
    final_part, final_scale = upper_root(every_part, every_scale, upper_transition, upper_children)
    weighted = site_loglik(final_part, final_scale, own_weights, taxa_total)
    overall = by_axis(jnp.sum(weighted), SITE_CLADE)
    return (weighted, overall / (site_count * lax.axis_size(SITE)))


def solution(mesh):
    torus = Mesh(mesh.devices.reshape(4, 8, 8, 2), ("site_0", "site_1", "clade_0", "clade_1"))
    return jax.shard_map(
        per_device,
        mesh=torus,
        in_specs=(P(CLADE, SITE), P(CLADE, None, None, None), P(CLADE, None), P(), P(), P(SITE)),
        out_specs=(P(SITE_CLADE), P()),
        check_vma=False,
    )
```

profile of v0, /device:TPU:1, one launch (start us, length us, event | category | flops | bytes accessed | tf_op | source)
XLA Modules:
  0.0 562.4 jit_solution(5683494163116401876)
XLA Ops:
  0.6 1.1 broadcast_compare_fusion
  1.7 1.8 fusion.3
  3.5 1.1 copy.26
  4.7 2.1 broadcast_in_dim.37
  6.8 6.1 %concatenate.9 = f32[63,4,4,4096]{3,2,1,0:T(4,128)} pad(f32[32,4,4,4096]{3,2,1,0:T(4,128)S(1)} %broadcast_in_dim.37, f32[]{:T(128)} %constant.221.clone.1), padding=0_31x0_0x0_0x0_0 | pad | bytes 24903684 | tf_op jit(solution)/shard_map/concatenate | solution.py:85
  12.9 331.2 %while.34 = (s32[]{:T(128)}, f32[63,4,4,4096]{3,2,1,0:T(4,128)}, f32[63,4096]{1,0:T(8,128)S(1)}, s32[31,2]{0,1:T(2,128)S(1)}, f32[62,4,4,4]{3,2,1,0:T(4,128)S(1)...) while((s32[]{:T(128)}, f32[63,4,4,4096]{3,2,1,0:T(4,128)}, ...), condition=%wide.region_2.3_spmd, body=%wide.region_0.2_spmd.sunk | while | flops 2101264 | bytes 4623685 | solution.py:70
  17.1 1.1 dynamic-slice_bitcast_fusion.12
  27.8 1.1 dynamic-slice_bitcast_fusion.12
  38.5 1.1 dynamic-slice_bitcast_fusion.12
  43.5 1.1 divide_dynamic-update-slice_fusion.4
  49.2 1.1 dynamic-slice_bitcast_fusion.12
  54.2 1.1 divide_dynamic-update-slice_fusion.4
  59.9 1.1 dynamic-slice_bitcast_fusion.12
  70.6 1.1 dynamic-slice_bitcast_fusion.12
  75.5 1.1 divide_dynamic-update-slice_fusion.4
  81.3 1.1 dynamic-slice_bitcast_fusion.12
  91.9 1.1 dynamic-slice_bitcast_fusion.12
  102.6 1.1 dynamic-slice_bitcast_fusion.12
  107.6 1.1 divide_dynamic-update-slice_fusion.4
  113.3 1.1 dynamic-slice_bitcast_fusion.12
  124.0 1.1 dynamic-slice_bitcast_fusion.12
  134.7 1.1 dynamic-slice_bitcast_fusion.12
  145.4 1.1 dynamic-slice_bitcast_fusion.12
  156.0 1.1 dynamic-slice_bitcast_fusion.12
  166.7 1.1 dynamic-slice_bitcast_fusion.12
  177.4 1.1 dynamic-slice_bitcast_fusion.12
  188.1 1.1 dynamic-slice_bitcast_fusion.12
  198.8 1.1 dynamic-slice_bitcast_fusion.12
  209.4 1.1 dynamic-slice_bitcast_fusion.12
  214.4 1.1 divide_dynamic-update-slice_fusion.4
  220.1 1.1 dynamic-slice_bitcast_fusion.12
  230.8 1.1 dynamic-slice_bitcast_fusion.12
  241.5 1.1 dynamic-slice_bitcast_fusion.12
  252.2 1.1 dynamic-slice_bitcast_fusion.12
  262.8 1.1 dynamic-slice_bitcast_fusion.12
  273.5 1.1 dynamic-slice_bitcast_fusion.12
  344.8 7.6 %all-to-all-start.2 = ((f32[8,2,1,1,1,256]{5,1,4,3,2,0:T(2,128)}), f32[8,2,1,1,1,256]{5,1,4,3,2,0:T(2,128)S(1)}, u32[]{:S(2)}, u32[]{:S(2)}) async-start(f32[8,2,1,1,1,256]{5,1,4,3,2,0:T(2,128)} %reshape_transpose_reshape_reshape_squeeze.3), calls=%async_computation.2 | async-start | bytes 32768 | tf_op jit(solution)/shard_map/all_to_all | solution.py:29
  354.1 5.0 all-to-all-done.2
  359.1 6.9 %all_to_all.20 = f32[8,2,1,1,1,256]{5,0,4,3,2,1:T(8,128)S(1)} all-to-all(f32[8,2,1,1,1,256]{5,0,4,3,2,1:T(8,128)S(1)} %copy.30), channel_id=1, replica_groups=mesh['site_0'=4,'site_1'=8,'clade_0'=8,'clade_1'=2] {'clade_1'}, dimensions={1} | all-to-all | bytes 32768 | tf_op jit(solution)/shard_map/all_to_all | solution.py:29
  366.0 3.4 all-to-all-start
  369.7 12.0 %all-to-all-done = f32[8,2,1,4,4,256]{5,4,3,1,2,0:T(4,128)S(1)} async-done(((f32[8,2,1,4,4,256]{5,4,3,1,2,0:T(4,128)}), f32[8,2,1,4,4,256]{5,4,3,1,2,0:T(4,128)S(1)}, u32[]{:S(2)}, u32[]{:S(2)}) %all-to-all-start) | async-done | bytes 262176 | tf_op jit(solution)/shard_map/all_to_all | solution.py:29
  381.7 4.1 all_to_all.21
  385.9 120.9 %while.35 = (s32[]{:T(128)}, f32[31,4,4,256]{3,2,1,0:T(4,128)S(1)}, f32[31,256]{1,0:T(8,128)S(1)}, s32[15,2]{0,1:T(2,128)S(1)}, f32[30,4,4,4]{3,2,1,0:T(4,128)S(...) while((s32[]{:T(128)}, f32[31,4,4,256]{3,2,1,0:T(4,128)S(1)}, ...), condition=%wide.region_5.6_spmd, body=%wide.region_3.5_spmd.sunk | while | flops 131344 | bytes 308037 | solution.py:70
  506.8 1.9 fusion.4
  508.7 7.7 %psum.28 = f32[]{:T(128)} all-reduce(f32[]{:T(128)} %get-tuple-element.358), channel_id=1, replica_groups=mesh['site_0'=4,'site_1'=8,'clade_0'=8,'clade_1'=2] {'site_0'}, use_global_device_ids=true, to_apply=%region_8.9 | all-reduce | flops 1 | bytes 8 | tf_op jit(solution)/shard_map/psum | solution.py:40
  516.4 20.0 %psum.29 = f32[]{:T(128)} all-reduce(f32[]{:T(128)} %psum.28), channel_id=1, replica_groups=mesh['site_0'=4,'site_1'=8,'clade_0'=8,'clade_1'=2] {'site_1'}, use_global_device_ids=true, to_apply=%region_9.10 | all-reduce | flops 1 | bytes 8 | tf_op jit(solution)/shard_map/psum | solution.py:40
  536.4 11.6 %psum.30 = f32[]{:T(128)} all-reduce(f32[]{:T(128)} %psum.29), channel_id=1, replica_groups=mesh['site_0'=4,'site_1'=8,'clade_0'=8,'clade_1'=2] {'clade_0'}, use_global_device_ids=true, to_apply=%region_10.11 | all-reduce | flops 1 | bytes 8 | tf_op jit(solution)/shard_map/psum | solution.py:40
  548.0 12.6 %psum.31 = f32[]{:T(128)} all-reduce(f32[]{:T(128)} %psum.30), channel_id=1, replica_groups=mesh['site_0'=4,'site_1'=8,'clade_0'=8,'clade_1'=2] {'clade_1'}, use_global_device_ids=true, to_apply=%region_11.12 | all-reduce | flops 1 | bytes 8 | tf_op jit(solution)/shard_map/psum | solution.py:40
  (819 shorter events, 131.3 us)
Async XLA Ops:
  4.7 8.3 %copy-start.1 = (s32[31,2]{0,1:T(2,128)S(1)}, s32[31,2]{0,1:T(2,128)}, u32[]{:S(2)}) copy-start(s32[31,2]{0,1:T(2,128)} %param.12) | copy-start | bytes 748
  12.8 356.5 %copy-start = (f32[30,4,4,4]{0,3,2,1:T(4,128)S(1)}, f32[30,4,4,4]{0,3,2,1:T(4,128)}, u32[]{:S(2)}) copy-start(f32[30,4,4,4]{0,3,2,1:T(4,128)} %param.13) | copy-start | bytes 23044
  12.9 373.0 %copy-start.2 = (s32[15,2]{0,1:T(2,128)S(1)}, s32[15,2]{0,1:T(2,128)}, u32[]{:S(2)}) copy-start(s32[15,2]{0,1:T(2,128)} %param.14) | copy-start | bytes 364
  344.8 14.3 %all-to-all-start.2 = ((f32[8,2,1,1,1,256]{5,1,4,3,2,0:T(2,128)}), f32[8,2,1,1,1,256]{5,1,4,3,2,0:T(2,128)S(1)}, u32[]{:S(2)}, u32[]{:S(2)}) async-start(f32[8,2,1,1,1,256]{5,1,4,3,2,0:T(2,128)} %reshape_transpose_reshape_reshape_squeeze.3), calls=%async_computation.2 | async-start | bytes 32768 | tf_op jit(solution)/shard_map/all_to_all | solution.py:29
  366.0 15.7 %all-to-all-start = ((f32[8,2,1,4,4,256]{5,4,3,1,2,0:T(4,128)}), f32[8,2,1,4,4,256]{5,4,3,1,2,0:T(4,128)S(1)}, u32[]{:S(2)}, u32[]{:S(2)}) async-start(f32[8,2,1,4,4,256]{5,4,3,1,2,0:T(4,128)} %bitcast.15), calls=%async_computation | async-start | bytes 524288 | tf_op jit(solution)/shard_map/all_to_all | solution.py:29
where the time goes:
time: 568 us; the launch traced here: 562 us
  loops' own time  291 us (51%)
  local copies, waits for them, and re-layouts  123 us (22%)
  blocking collectives  62.9 us (11%)
  other arithmetic  54.9 us (10%)
  waiting for transfers between devices  16.9 us (3%)
  starting transfers between devices  11 us (2%)
    another operation x2, loops' own time, prune_tree(): return lax.fori_loop(0, merges.shape[0], advance, (partials, scales))  291 us
    psum x4, blocking collectives, by_axis(): return functools.reduce(lax.psum, axes, shard)  52 us
    dynamic_update_slice x46, other arithmetic, advance(): lax.dynamic_update_index_in_dim(cur_parts, product / biggest, target, 0)  34.6 us
    squeeze x46, local copies, waits for them, and re-layouts, advance(): lax.dynamic_index_in_dim(cur_parts, left_index, 0, keepdims=False)  33.3 us
    dynamic_slice x46, local copies, waits for them, and re-layouts, advance(): left_index = merges[node_index, 0]  28.2 us
    slice x92, local copies, waits for them, and re-layouts, transform(): total = matrix[:, :, 0, None] * values_in[:, 0, None, :]  23.8 us
    all_to_all x2, waiting for transfers between devices, turned_blocks(): lax.all_to_all(blocks, axes[k], split_axis=k, concat_axis=k, tiled=True)  16.9 us
    reduce_max x46, other arithmetic, advance(): biggest = jnp.max(product, axis=(0, 1))  14.1 us
  transfers between devices with their start and end apart: 2, of which 2 were waited for; matrix products, arithmetic and copies ran while one was open for 0% of the time, Pallas kernels for 0%

commit v1 on v0

v1 whole, which is shorter than its diff:
```python
import jax
import jax.numpy as jnp
from jax import lax
from jax.experimental import pallas as pl
from jax.experimental.pallas import tpu as pltpu
from jax.sharding import Mesh
from jax.sharding import PartitionSpec as P

CLADE = ("clade_0", "clade_1")
SITE = ("site_0", "site_1")
SITE_CLADE = SITE + CLADE


def splat(column_block, k):
    return jnp.broadcast_to(column_block[:, k : k + 1], (8, 128))


def clade_kernel(merges_ref, probs_ref, tips_ref, tables_ref, out_ref, parts_ref, inv_ref, log_ref):
    merges = merges_ref.shape[0] // 2
    leaves = merges + 1
    groups = out_ref.shape[0] // 32
    tiles = range(2 * groups // 8)
    log_ref[...] = jnp.zeros_like(log_ref)

    def codes(taxon):
        start = (taxon // 8) * (16 * groups) + taxon % 8
        halves = [tips_ref[pl.ds(start + 8 * h, groups, stride=16), :] for h in range(2)]
        return [half[8 * i : 8 * i + 8] for half in halves for i in range(groups // 8)]

    def leaf_branch(taxon):
        idx = codes(taxon)
        table = tables_ref[taxon]

        def planes(rate):
            for state in range(4):
                column = splat(table, rate * 4 + state)
                yield [
                    jnp.take_along_axis(column, idx[t], axis=0, mode="promise_in_bounds")
                    for t in tiles
                ]

        return planes

    def inner_branch(node):
        inner = node - leaves
        inv = [inv_ref[inner, 8 * t : 8 * t + 8, :] for t in tiles]

        def planes(rate):
            part = [
                [
                    parts_ref[inner * 16 + rate * 4 + b, 8 * t : 8 * t + 8, :] * inv[t]
                    for t in tiles
                ]
                for b in range(4)
            ]
            for state in range(4):
                p = [probs_ref[node * 64 + rate * 16 + state * 4 + b] for b in range(4)]
                yield [
                    (p[0] * part[0][t] + p[1] * part[1][t])
                    + (p[2] * part[2][t] + p[3] * part[3][t])
                    for t in tiles
                ]

        return planes

    def combine(j, one, other, keep):
        biggest = None
        for rate in range(4):
            for state, (u, v) in enumerate(zip(one(rate), other(rate))):
                q = [u[t] * v[t] for t in tiles]
                keep(rate, state, q)
                biggest = q if biggest is None else [jnp.maximum(biggest[t], q[t]) for t in tiles]
        return biggest

    def merge(j, high, low):
        def keep(rate, state, q):
            for t in tiles:
                parts_ref[j * 16 + rate * 4 + state, 8 * t : 8 * t + 8, :] = q[t]

        def run(one, other):
            biggest = combine(j, one(high), other(low), keep)
            for t in tiles:
                rows = slice(8 * t, 8 * t + 8)
                inv = pl.reciprocal(biggest[t], approx=True)
                inv_ref[j, rows, :] = inv
                log_ref[rows, :] = log_ref[rows, :] - jnp.log(inv)

        pl.when(high < leaves)(lambda: run(leaf_branch, leaf_branch))
        pl.when((high >= leaves) & (low < leaves))(lambda: run(inner_branch, leaf_branch))
        pl.when(low >= leaves)(lambda: run(inner_branch, inner_branch))

    def step(j, _):
        c, d = merges_ref[2 * j], merges_ref[2 * j + 1]
        merge(j, jnp.maximum(c, d), jnp.minimum(c, d))
        return 0

    lax.fori_loop(0, merges, step, 0)

    last = merges - 1
    for t in tiles:
        rows = slice(8 * t, 8 * t + 8)
        h, first = divmod(8 * t, groups)
        scale = log_ref[rows, :] + jnp.log(inv_ref[last, rows, :])
        for rate in range(4):
            for state in range(4):
                value = jnp.log(parts_ref[last * 16 + rate * 4 + state, rows, :]) + scale
                out_ref[pl.ds(first * 32 + state * 8 + rate * 2 + h, 8, stride=32), :] = value


def upper_kernel(total_taxa, merges_ref, roots_ref, probs_ref, weights_ref, out_ref, sum_ref, parts_ref):
    merges = merges_ref.shape[0] // 2
    clades = merges + 1

    def over_rates(op, x):
        x = op(x, pltpu.roll(x, 2, 0))
        return op(x, pltpu.roll(x, 4, 0))

    scale = jnp.zeros((8, 128), jnp.float32)
    for k in range(clades):
        rows = [roots_ref[k * 32 + 8 * a : k * 32 + 8 * a + 8, :] for a in range(4)]
        top = jnp.maximum(jnp.maximum(rows[0], rows[1]), jnp.maximum(rows[2], rows[3]))
        top = over_rates(jnp.maximum, top)
        scale = scale + top
        for a in range(4):
            parts_ref[k, 8 * a : 8 * a + 8, :] = jnp.exp(rows[a] - top)

    def branch(node):
        part = [parts_ref[node, 8 * b : 8 * b + 8, :] for b in range(4)]
        block = probs_ref[node]
        out = []
        for a in range(4):
            p = [splat(block, a * 4 + b) for b in range(4)]
            out.append((p[0] * part[0] + p[1] * part[1]) + (p[2] * part[2] + p[3] * part[3]))
        return out

    for j in range(merges):
        u, v = branch(merges_ref[2 * j]), branch(merges_ref[2 * j + 1])
        q = [u[a] * v[a] for a in range(4)]
        if j < merges - 1:
            top = jnp.maximum(jnp.maximum(q[0], q[1]), jnp.maximum(q[2], q[3]))
            inv = pl.reciprocal(over_rates(jnp.maximum, top), approx=True)
            scale = scale - jnp.log(inv)
            for a in range(4):
                parts_ref[clades + j, 8 * a : 8 * a + 8, :] = q[a] * inv
        else:
            top = over_rates(jnp.maximum, jnp.maximum(jnp.maximum(q[0], q[1]), jnp.maximum(q[2], q[3])))
            inv = pl.reciprocal(top, approx=True)
            scale = scale - jnp.log(inv)
            total = over_rates(jnp.add, ((q[0] + q[1]) + (q[2] + q[3])) * inv)
    loglik = (jnp.log(total * (1.0 / 16.0)) + scale)[0:2, :]
    weighted = weights_ref[...].astype(jnp.float32) * loglik * (1.0 / total_taxa)
    out_ref[...] = weighted
    sum_ref[...] = jnp.broadcast_to(weighted[0:1, :] + weighted[1:2, :], sum_ref.shape)


def sum_over(rows, axes, copies):
    got = lax.all_to_all(rows, axes, split_axis=0, concat_axis=0, tiled=True)
    return jnp.broadcast_to(jnp.sum(got, axis=0, keepdims=True), (copies,) + got.shape[1:])


def per_device(tips, transition, clade_children, upper_transition, upper_children, pattern_weights):
    leaves, sites = tips.shape
    clades = lax.axis_size(CLADE)
    groups = lax.axis_size(SITE)
    position = lax.axis_index(CLADE)
    piece = sites // clades
    nodes = transition.shape[0]
    vmem = pl.BlockSpec(memory_space=pltpu.VMEM)
    smem = pl.BlockSpec(memory_space=pltpu.SMEM)

    tiled = tips.reshape(leaves // 8, 8, sites // 128, 128).transpose(0, 2, 1, 3)
    tiled = tiled.reshape(leaves * sites // 128, 128)
    by_code = transition[:leaves].reshape(leaves, 16, 4)
    gap = jnp.sum(by_code, axis=2, keepdims=True)
    tables = jnp.concatenate([by_code, gap, jnp.zeros((leaves, 16, 3), jnp.float32)], axis=2)
    tables = tables.transpose(0, 2, 1)
    logs = pl.pallas_call(
        clade_kernel,
        out_shape=jax.ShapeDtypeStruct((clades * 32, 128), jnp.float32),
        in_specs=[smem, smem, vmem, vmem],
        out_specs=vmem,
        scratch_shapes=[
            pltpu.VMEM(((leaves - 1) * 16, sites // 128, 128), jnp.float32),
            pltpu.VMEM((leaves - 1, sites // 128, 128), jnp.float32),
            pltpu.VMEM((sites // 128, 128), jnp.float32),
        ],
        name="clade",
    )(clade_children.reshape(-1), transition.reshape(-1), tiled, tables)

    got = lax.all_to_all(
        logs.reshape(clades, 32, 128), CLADE, split_axis=0, concat_axis=0, tiled=True
    )
    upper = upper_transition.reshape(-1, 4, 16)
    upper = jnp.repeat(upper, 2, axis=1)
    own = lax.dynamic_slice_in_dim(pattern_weights, position * piece, piece, 0)
    weighted, addend = pl.pallas_call(
        lambda *refs: upper_kernel(float(leaves * clades), *refs),
        out_shape=[
            jax.ShapeDtypeStruct((piece // 128, 128), jnp.float32),
            jax.ShapeDtypeStruct((clades, 128), jnp.float32),
        ],
        in_specs=[smem, vmem, vmem, vmem],
        out_specs=[vmem, vmem],
        scratch_shapes=[pltpu.VMEM((2 * clades - 1, 32, 128), jnp.float32)],
        name="upper",
    )(upper_children.reshape(-1), got.reshape(clades * 32, 128), upper, own.reshape(piece // 128, 128))

    part = sum_over(addend.reshape(clades, 1, 128), CLADE, groups)
    whole = sum_over(part, SITE, 1)
    return weighted.reshape(piece), jnp.sum(whole) / (sites * groups)


def solution(mesh):
    torus = Mesh(mesh.devices.reshape(4, 8, 8, 2), SITE_CLADE)
    return jax.shard_map(
        per_device,
        mesh=torus,
        in_specs=(P(CLADE, SITE), P(CLADE, None, None, None), P(CLADE, None), P(), P(), P(SITE)),
        out_specs=(P(SITE_CLADE), P()),
        check_vma=False,
    )
```

time: 568 us -> 71 us (0.12)
  loops' own time: 291 us -> 0 us
  local copies, waits for them, and re-layouts: 123 us -> 6.73 us
  other arithmetic: 54.9 us -> 1.41 us
  blocking collectives: 62.9 us -> 29.7 us
  Pallas kernels: 0 us -> 10.4 us
  waiting for transfers between devices: 16.9 us -> 9.6 us
    another operation x2 -> x0, loops' own time: 291 us -> none  [prune_tree(): return lax.fori_loop(0, merges.shape[0], advance, (partials, scales))]
    psum x4 -> x0, blocking collectives: 52 us -> none  [by_axis(): return functools.reduce(lax.psum, axes, shard)]
    dynamic_update_slice x46 -> x0, other arithmetic: 34.6 us -> none  [advance(): lax.dynamic_update_index_in_dim(cur_parts, product / biggest, target, 0)]
    squeeze x92 -> x0, local copies, waits for them, and re-layouts: 33.7 us -> none  [the longest x46 33.3 us: advance(): lax.dynamic_index_in_dim(cur_parts, left_index, 0, keepdims=False)]
    dynamic_slice x46 -> x0, local copies, waits for them, and re-layouts: 28.2 us -> none  [advance(): left_index = merges[node_index, 0]]
    slice x95 -> x0, local copies, waits for them, and re-layouts: 24.8 us -> none  [the longest x92 23.8 us: transform(): total = matrix[:, :, 0, None] * values_in[:, 0, None, :]]
    all_to_all x2, blocking collectives: 10.9 us -> 29.7 us  [sum_over(): got = lax.all_to_all(rows, axes, split_axis=0, concat_axis=0, tiled=True)]
    reduce_max x46 -> x0, other arithmetic: 14.1 us -> none  [advance(): biggest = jnp.max(product, axis=(0, 1))]
  transfers between devices with their start and end apart: 2 -> 1, of which waited for: 2 -> 1; matrix products, arithmetic and copies ran while one was open for 0% -> 2% of each run, Pallas kernels for 0% -> 0%
where the time goes in v1:
time: 71 us; the launch traced here: 70.5 us
  blocking collectives  29.7 us (42%)
  Pallas kernels  10.4 us (15%)
  starting transfers between devices  10.3 us (15%)
  waiting for transfers between devices  9.6 us (14%)
  local copies, waits for them, and re-layouts  6.73 us (9%)
  between operations  2.49 us (4%)
  other arithmetic  1.41 us (2%)
    all_to_all x2, blocking collectives, sum_over(): got = lax.all_to_all(rows, axes, split_axis=0, concat_axis=0, tiled=True)  29.7 us
    all_to_all x1, starting transfers between devices, per_device(): lax.all_to_all(logs.reshape(clades, 32, 128), CLADE, split_axis=0, concat...  10.3 us
    all_to_all x1, waiting for transfers between devices, per_device(): lax.all_to_all(logs.reshape(clades, 32, 128), CLADE, split_axis=0, concat...  9.6 us
    pallas_call x1, Pallas kernels, per_device(): pl.pallas_call(clade_kernel, out_shape=jax.ShapeDtypeStruct((clades * 32,...  7.78 us
    unnamed x15, local copies, waits for them, and re-layouts  2.71 us
    pallas_call x1, Pallas kernels, per_device(): pl.pallas_call(lambda *refs: upper_kernel(float(leaves * clades), *refs),...  2.58 us
  transfers between devices with their start and end apart: 1, of which 1 were waited for; matrix products, arithmetic and copies ran while one was open for 2% of the time, Pallas kernels for 0%

profile of v1, /device:TPU:1, one launch (start us, length us, event | category | flops | bytes accessed | tf_op | source)
XLA Modules:
  0.0 70.5 jit_solution(11503457289238376334)
XLA Ops:
  0.6 0.0 copy-start
  0.6 0.0 copy-start.2
  0.7 1.2 %copy.37 = f32[62,4,4,4]{3,2,1,0:T(4,128)S(1)} copy(f32[62,4,4,4]{0,3,2,1:T(4,128)} %param.7) | data formatting | bytes 31744 | tf_op args[1]
  1.8 0.0 copy-done.2
  1.9 0.0 copy-start.4
  1.9 0.6 copy-done.4
  2.5 0.1 copy.36
  2.6 0.6 reshape.53.merges_ref
  3.3 1.1 %reshape.54.probs_ref = f32[3968]{0:T(1024)} reshape(f32[62,4,4,4]{3,2,1,0:T(4,128)S(1)} %copy.37) | data formatting | bytes 31744 | tf_op jit(solution)/shard_map/reshape | solution.py:188
  4.3 0.1 copy.40
  4.4 0.1 copy.39
  4.5 0.1 pad.2.clone
  4.6 0.7 %maximum_bitcast_fusion.tables_ref = f32[32,8,16]{2,1,0:T(8,128)} fusion(f32[32,16,1]{1,2,0:T(1,128)S(1)} %copy.40, f32[32,16,4]{1,2,0:T(4,128)S(1)} %copy.39, f32[8]{0:T(128)S(1)} %pad.2.clone), kind=kLoop, calls=%fused_computation | loop fusion | flops 8192 | bytes 26656 | tf_op jit(solution)/shard_map/transpose | solution.py:176
  5.3 7.8 %clade.1 = f32[512,128]{1,0:T(8,128)} custom-call(s32[62]{0:T(128)} %reshape.53.merges_ref, f32[3968]{0:T(1024)} %reshape.54.probs_ref, s32[1024,128]{1,0:T(8,128)} %bitcast.22, f32[32,8,16]{2,1,0:T(8,128)} %maximum_bitcast_fusion.tables_ref), custom_call_target="tpu_custom_call" | custom-call | tf_op jit(solution)/shard_map/clade/pallas_call | solution.py:177
  13.1 0.0 copy-start.3
  13.1 10.3 %all-to-all-start = ((f32[16,32,128]{2,1,0:T(8,128)}), f32[16,32,128]{2,1,0:T(8,128)S(1)}, u32[]{:S(2)}, u32[]{:S(2)}) async-start(f32[16,32,128]{2,1,0:T(8,128)} %bitcast.20), calls=%async_computation | async-start | bytes 524288 | tf_op jit(solution)/shard_map/all_to_all | solution.py:190
  23.4 0.0 copy-start.5
  23.4 0.7 copy-done.5
  24.0 0.1 copy.35
  24.1 0.6 reshape.52.refs_0_
  24.7 0.0 copy-done.3
  24.7 0.1 copy.41
  24.8 0.0 copy-done
  24.8 0.7 dynamic-slice_bitcast_fusion.refs_3_
  25.5 9.6 %all-to-all-done = f32[16,32,128]{2,1,0:T(8,128)S(1)} async-done(((f32[16,32,128]{2,1,0:T(8,128)}), f32[16,32,128]{2,1,0:T(8,128)S(1)}, u32[]{:S(2)}, u32[]{:S(2)}) %all-to-all-start) | async-done | bytes 262176 | tf_op jit(solution)/shard_map/all_to_all | solution.py:190
  35.1 0.0 copy-start.1
  35.1 0.7 %broadcast_in_dim.18 = f32[30,4,2,16]{3,2,1,0:T(2,128)} broadcast(f32[30,4,16]{2,1,0:T(4,128)S(1)} %copy.41), dimensions={0,1,3} | broadcast | bytes 23040 | tf_op jit(solution)/shard_map/broadcast_in_dim | solution.py:194
  35.8 0.0 copy-done.1
  35.8 2.6 %upper.1 = (f32[2,128]{1,0:T(2,128)}, f32[16,128]{1,0:T(8,128)}) custom-call(s32[30]{0:T(128)} %reshape.52.refs_0_, f32[512,128]{1,0:T(8,128)} %bitcast.21, f32[30,8,16]{2,1,0:T(8,128)} %bitcast.23, s32[2,128]{1,0:T(2,128)} %dynamic-slice_bitcast_fusion.refs_3_), custom_call_target="tpu_custom_call" | custom-call | tf_op jit(solution)/shard_map/upper/pallas_call | solution.py:196
  38.4 9.9 %all_to_all.15 = f32[16,1,128]{2,1,0:T(1,128)S(1)} all-to-all(f32[16,1,128]{2,1,0:T(1,128)} %bitcast.28), channel_id=1, replica_groups=mesh['site_0'=4,'site_1'=8,'clade_0'=8,'clade_1'=2] {'clade_0','clade_1'}, dimensions={0} | all-to-all | bytes 16384 | tf_op jit(solution)/shard_map/all_to_all | solution.py:157
  48.4 19.8 %all_to_all.16 = f32[32,1,128]{2,1,0:T(1,128)S(1)} all-to-all(f32[32,1,128]{2,1,0:T(1,128)S(1)} %broadcast_in_dim.19), channel_id=1, replica_groups=mesh['site_0'=4,'site_1'=8,'clade_0'=8,'clade_1'=2] {'site_0','site_1'}, dimensions={0} | all-to-all | bytes 32768 | tf_op jit(solution)/shard_map/all_to_all | solution.py:157
  68.1 0.6 reduce_sum.33
  (4 shorter events, 0.1 us)
Async XLA Ops:
  0.6 24.2 %copy-start = (s32[4096]{0:T(1024)S(1)}, s32[4096]{0:T(1024)}, u32[]{:S(2)}) copy-start(s32[4096]{0:T(1024)} %param.11) | copy-start | bytes 49156
  0.6 1.2 %copy-start.2 = (f32[62,4,4,4]{0,3,2,1:T(4,128)S(1)}, f32[62,4,4,4]{0,3,2,1:T(4,128)}, u32[]{:S(2)}) copy-start(f32[62,4,4,4]{0,3,2,1:T(4,128)} %param.7) | copy-start | bytes 47620
  1.9 0.7 copy-start.4
  13.1 11.6 %copy-start.3 = (f32[30,4,4,4]{0,3,2,1:T(4,128)S(1)}, f32[30,4,4,4]{0,3,2,1:T(4,128)}, u32[]{:S(2)}) copy-start(f32[30,4,4,4]{0,3,2,1:T(4,128)} %param.9) | copy-start | bytes 23044
  13.1 22.0 %all-to-all-start = ((f32[16,32,128]{2,1,0:T(8,128)}), f32[16,32,128]{2,1,0:T(8,128)S(1)}, u32[]{:S(2)}, u32[]{:S(2)}) async-start(f32[16,32,128]{2,1,0:T(8,128)} %bitcast.20), calls=%async_computation | async-start | bytes 524288 | tf_op jit(solution)/shard_map/all_to_all | solution.py:190
  23.4 0.7 copy-start.5
  35.1 0.7 %copy-start.1 = (f32[16,32,128]{2,1,0:T(8,128)}, f32[16,32,128]{2,1,0:T(8,128)S(1)}, u32[]{:S(2)}) copy-start(f32[16,32,128]{2,1,0:T(8,128)S(1)} %all-to-all-done) | copy-start | bytes 786436

commit v2 on v1

--- a/solution.py
+++ b/solution.py
@@ -15,12 +15,42 @@
     return jnp.broadcast_to(column_block[:, k : k + 1], (8, 128))
 
 
-def clade_kernel(merges_ref, probs_ref, tips_ref, tables_ref, out_ref, parts_ref, inv_ref, log_ref):
-    merges = merges_ref.shape[0] // 2
+def by_row(rows):
+    shape = (8, rows[0].shape[1])
+    sublane = lax.broadcasted_iota(jnp.int32, shape, 0)
+    block = jnp.broadcast_to(rows[-1], shape)
+    for s in reversed(range(len(rows) - 1)):
+        block = jnp.where(sublane <= s, jnp.broadcast_to(rows[s], shape), block)
+    return block
+
+
+def clade_kernel(
+    merges_hbm, rows_hbm, tips_hbm, out_hbm,
+    merges_ref, probs_ref, rows_ref, tips_ref, tables_ref, parts_ref, inv_ref, log_ref, root_ref, sems,
+):
+    copies = [
+        pltpu.make_async_copy(source, target, sems.at[i])
+        for i, (source, target) in enumerate(
+            [(rows_hbm, rows_ref), (merges_hbm, merges_ref), (rows_hbm, probs_ref), (tips_hbm, tips_ref)]
+        )
+    ]
+    for copy in copies:
+        copy.start()
+    merges = merges_ref.shape[1]
     leaves = merges + 1
-    groups = out_ref.shape[0] // 32
+    groups = out_hbm.shape[0] // 32
     tiles = range(2 * groups // 8)
     log_ref[...] = jnp.zeros_like(log_ref)
+    copies[0].wait()
+    blocks = []
+    for k in range(16):
+        rows = [rows_ref[4 * k + b : 4 * k + b + 1, :] for b in range(4)]
+        blocks.append(by_row(rows + [(rows[0] + rows[1]) + (rows[2] + rows[3])]))
+    for taxon in range(leaves):
+        for k in range(16):
+            tables_ref[taxon * 16 + k] = splat(blocks[k], taxon)
+    for copy in copies[1:]:
+        copy.wait()
 
     def codes(taxon):
         start = (taxon // 8) * (16 * groups) + taxon % 8
@@ -29,11 +59,10 @@
 
     def leaf_branch(taxon):
         idx = codes(taxon)
-        table = tables_ref[taxon]
 
         def planes(rate):
             for state in range(4):
-                column = splat(table, rate * 4 + state)
+                column = tables_ref[taxon * 16 + rate * 4 + state]
                 yield [
                     jnp.take_along_axis(column, idx[t], axis=0, mode="promise_in_bounds")
                     for t in tiles
@@ -54,7 +83,7 @@
                 for b in range(4)
             ]
             for state in range(4):
-                p = [probs_ref[node * 64 + rate * 16 + state * 4 + b] for b in range(4)]
+                p = [probs_ref[rate * 16 + state * 4 + b, node] for b in range(4)]
                 yield [
                     (p[0] * part[0][t] + p[1] * part[1][t])
                     + (p[2] * part[2][t] + p[3] * part[3][t])
@@ -63,52 +92,61 @@
 
         return planes
 
-    def combine(j, one, other, keep):
+    def merge(j, one, other):
         biggest = None
         for rate in range(4):
-            for state, (u, v) in enumerate(zip(one(rate), other(rate))):
+            firsts = list(one(rate))
+            for state, (u, v) in enumerate(zip(firsts, other(rate))):
                 q = [u[t] * v[t] for t in tiles]
-                keep(rate, state, q)
+                for t in tiles:
+                    parts_ref[j * 16 + rate * 4 + state, 8 * t : 8 * t + 8, :] = q[t]
                 biggest = q if biggest is None else [jnp.maximum(biggest[t], q[t]) for t in tiles]
-        return biggest
-
-    def merge(j, high, low):
-        def keep(rate, state, q):
-            for t in tiles:
-                parts_ref[j * 16 + rate * 4 + state, 8 * t : 8 * t + 8, :] = q[t]
-
-        def run(one, other):
-            biggest = combine(j, one(high), other(low), keep)
-            for t in tiles:
-                rows = slice(8 * t, 8 * t + 8)
-                inv = pl.reciprocal(biggest[t], approx=True)
-                inv_ref[j, rows, :] = inv
-                log_ref[rows, :] = log_ref[rows, :] - jnp.log(inv)
-
-        pl.when(high < leaves)(lambda: run(leaf_branch, leaf_branch))
-        pl.when((high >= leaves) & (low < leaves))(lambda: run(inner_branch, leaf_branch))
-        pl.when(low >= leaves)(lambda: run(inner_branch, inner_branch))
+        for t in tiles:
+            rows = slice(8 * t, 8 * t + 8)
+            inv = pl.reciprocal(biggest[t], approx=True)
+            inv_ref[j, rows, :] = inv
+            log_ref[rows, :] = log_ref[rows, :] - jnp.log(inv)
 
     def step(j, _):
-        c, d = merges_ref[2 * j], merges_ref[2 * j + 1]
-        merge(j, jnp.maximum(c, d), jnp.minimum(c, d))
+        c, d = merges_ref[0, j], merges_ref[1, j]
+        leaf, inner = leaf_branch, inner_branch
+        high, low = jnp.maximum(c, d), jnp.minimum(c, d)
+        pl.when(high < leaves)(lambda: merge(j, leaf(high), leaf(low)))
+        pl.when((high >= leaves) & (low < leaves))(lambda: merge(j, inner(high), leaf(low)))
+        pl.when(low >= leaves)(lambda: merge(j, inner(high), inner(low)))
         return 0
 
     lax.fori_loop(0, merges, step, 0)
 
     last = merges - 1
-    for t in tiles:
-        rows = slice(8 * t, 8 * t + 8)
-        h, first = divmod(8 * t, groups)
-        scale = log_ref[rows, :] + jnp.log(inv_ref[last, rows, :])
-        for rate in range(4):
-            for state in range(4):
-                value = jnp.log(parts_ref[last * 16 + rate * 4 + state, rows, :]) + scale
-                out_ref[pl.ds(first * 32 + state * 8 + rate * 2 + h, 8, stride=32), :] = value
+    half = 8 * 32
+    sends = []
+    for part in range(groups // 8):
+        for h in range(2):
+            rows = slice(h * groups + 8 * part, h * groups + 8 * part + 8)
+            scale = log_ref[rows, :] + jnp.log(inv_ref[last, rows, :])
+            for rate in range(4):
+                for state in range(4):
+                    value = jnp.log(parts_ref[last * 16 + rate * 4 + state, rows, :]) + scale
+                    start = part * half + state * 8 + rate * 2 + h
+                    root_ref[pl.ds(start, 8, stride=32), :] = value
+        span = pl.ds(part * half, half)
+        sends.append(pltpu.make_async_copy(root_ref.at[span], out_hbm.at[span], sems.at[4 + part]))
+        sends[-1].start()
+    for send in sends:
+        send.wait()
+
+
+def spread_kernel(rows_ref, out_ref):
+    for k in range(16):
+        rows = [rows_ref[16 * rate + k : 16 * rate + k + 1, :] for rate in range(4)]
+        block = by_row([row for row in rows for _ in range(2)])
+        for node in range(rows_ref.shape[1]):
+            out_ref[node * 16 + k] = splat(block, node)
 
 
 def upper_kernel(total_taxa, merges_ref, roots_ref, probs_ref, weights_ref, out_ref, sum_ref, parts_ref):
-    merges = merges_ref.shape[0] // 2
+    merges = merges_ref.shape[1]
     clades = merges + 1
 
     def over_rates(op, x):
@@ -126,15 +164,14 @@
 
     def branch(node):
         part = [parts_ref[node, 8 * b : 8 * b + 8, :] for b in range(4)]
-        block = probs_ref[node]
         out = []
         for a in range(4):
-            p = [splat(block, a * 4 + b) for b in range(4)]
+            p = [probs_ref[node * 16 + a * 4 + b] for b in range(4)]
             out.append((p[0] * part[0] + p[1] * part[1]) + (p[2] * part[2] + p[3] * part[3]))
         return out
 
     for j in range(merges):
-        u, v = branch(merges_ref[2 * j]), branch(merges_ref[2 * j + 1])
+        u, v = branch(merges_ref[0, j]), branch(merges_ref[1, j])
         q = [u[a] * v[a] for a in range(4)]
         if j < merges - 1:
             top = jnp.maximum(jnp.maximum(q[0], q[1]), jnp.maximum(q[2], q[3]))
@@ -170,28 +207,42 @@
 
     tiled = tips.reshape(leaves // 8, 8, sites // 128, 128).transpose(0, 2, 1, 3)
     tiled = tiled.reshape(leaves * sites // 128, 128)
-    by_code = transition[:leaves].reshape(leaves, 16, 4)
-    gap = jnp.sum(by_code, axis=2, keepdims=True)
-    tables = jnp.concatenate([by_code, gap, jnp.zeros((leaves, 16, 3), jnp.float32)], axis=2)
-    tables = tables.transpose(0, 2, 1)
+    rows = transition.transpose(1, 2, 3, 0).reshape(64, -1)
+    hbm = pl.BlockSpec(memory_space=pl.ANY)
+    merges = clade_children.T
     logs = pl.pallas_call(
         clade_kernel,
         out_shape=jax.ShapeDtypeStruct((clades * 32, 128), jnp.float32),
-        in_specs=[smem, smem, vmem, vmem],
-        out_specs=vmem,
+        in_specs=[hbm, hbm, hbm],
+        out_specs=hbm,
         scratch_shapes=[
+            pltpu.SMEM(merges.shape, jnp.int32),
+            pltpu.SMEM(rows.shape, jnp.float32),
+            pltpu.VMEM(rows.shape, jnp.float32),
+            pltpu.VMEM(tiled.shape, jnp.int32),
+            pltpu.VMEM((leaves * 16, 8, 128), jnp.float32),
             pltpu.VMEM(((leaves - 1) * 16, sites // 128, 128), jnp.float32),
             pltpu.VMEM((leaves - 1, sites // 128, 128), jnp.float32),
             pltpu.VMEM((sites // 128, 128), jnp.float32),
+            pltpu.VMEM((clades * 32, 128), jnp.float32),
+            pltpu.SemaphoreType.DMA((6,)),
         ],
         name="clade",
-    )(clade_children.reshape(-1), transition.reshape(-1), tiled, tables)
+    )(merges, rows, tiled)
 
     got = lax.all_to_all(
         logs.reshape(clades, 32, 128), CLADE, split_axis=0, concat_axis=0, tiled=True
     )
-    upper = upper_transition.reshape(-1, 4, 16)
-    upper = jnp.repeat(upper, 2, axis=1)
+    upper_rows = upper_transition.transpose(1, 2, 3, 0).reshape(64, -1)
+    spread = pl.pallas_call(
+        spread_kernel,
+        out_shape=jax.ShapeDtypeStruct((upper_rows.shape[1] * 16, 8, 128), jnp.float32),
+        in_specs=[vmem],
+        out_specs=vmem,
+        compiler_params=pltpu.CompilerParams(vmem_limit_bytes=8 << 20),
+        cost_estimate=pl.CostEstimate(flops=1 << 22, bytes_accessed=2 << 20, transcendentals=0),
+        name="spread",
+    )(upper_rows)
     own = lax.dynamic_slice_in_dim(pattern_weights, position * piece, piece, 0)
     weighted, addend = pl.pallas_call(
         lambda *refs: upper_kernel(float(leaves * clades), *refs),
@@ -202,8 +253,9 @@
         in_specs=[smem, vmem, vmem, vmem],
         out_specs=[vmem, vmem],
         scratch_shapes=[pltpu.VMEM((2 * clades - 1, 32, 128), jnp.float32)],
+        compiler_params=pltpu.CompilerParams(vmem_limit_bytes=8 << 20),
         name="upper",
-    )(upper_children.reshape(-1), got.reshape(clades * 32, 128), upper, own.reshape(piece // 128, 128))
+    )(upper_children.T, got.reshape(clades * 32, 128), spread, own.reshape(piece // 128, 128))
 
     part = sum_over(addend.reshape(clades, 1, 128), CLADE, groups)
     whole = sum_over(part, SITE, 1)

time: 71 us -> 63.8 us (0.90)
  local copies, waits for them, and re-layouts: 6.73 us -> 0.86 us
  other arithmetic: 1.41 us -> 0.64 us
    reshape x5 -> x0, local copies, waits for them, and re-layouts: 2.48 us -> none  [the longest x1 1.07 us: per_device(): transition.reshape(-1)]
    unnamed x15 -> x6, local copies, waits for them, and re-layouts: 2.71 us -> 0.77 us
    pallas_call x1, Pallas kernels: 2.58 us -> 1.61 us  [per_device(): pl.pallas_call(lambda *refs: upper_kernel(float(leaves * clades), *refs),...]
    pallas_call x0 -> x1, Pallas kernels: none -> 0.91 us  [per_device(): pl.pallas_call(spread_kernel, out_shape=jax.ShapeDtypeStruct((upper_rows....]
    broadcast_in_dim x3 -> x0, local copies, waits for them, and re-layouts: 0.8 us -> none  [the longest x1 0.73 us: per_device(): upper = jnp.repeat(upper, 2, axis=1)]
    transpose x1 -> x0, other arithmetic: 0.73 us -> none  [per_device(): tables = tables.transpose(0, 2, 1)]
  transfers between devices with their start and end apart: 1 -> 1, of which waited for: 1 -> 1; matrix products, arithmetic and copies ran while one was open for 2% -> 0% of each run, Pallas kernels for 0% -> 1%
where the time goes in v2:
time: 63.8 us; the launch traced here: 63.4 us
  blocking collectives  29.4 us (46%)
  starting transfers between devices  10.2 us (16%)
  waiting for transfers between devices  10 us (16%)
  Pallas kernels  9.88 us (15%)
  between operations  2.44 us (4%)
  local copies, waits for them, and re-layouts  0.86 us (1%)
  other arithmetic  0.64 us (1%)
    all_to_all x2, blocking collectives, sum_over(): got = lax.all_to_all(rows, axes, split_axis=0, concat_axis=0, tiled=True)  29.4 us
    all_to_all x1, starting transfers between devices, per_device(): lax.all_to_all(logs.reshape(clades, 32, 128), CLADE, split_axis=0, concat...  10.2 us
    all_to_all x1, waiting for transfers between devices, per_device(): lax.all_to_all(logs.reshape(clades, 32, 128), CLADE, split_axis=0, concat...  10 us
    pallas_call x1, Pallas kernels, per_device(): pl.pallas_call(clade_kernel, out_shape=jax.ShapeDtypeStruct((clades * 32,...  7.37 us
    pallas_call x1, Pallas kernels, per_device(): pl.pallas_call(lambda *refs: upper_kernel(float(leaves * clades), *refs),...  1.61 us
  transfers between devices with their start and end apart: 1, of which 1 were waited for; matrix products, arithmetic and copies ran while one was open for 0% of the time, Pallas kernels for 1%

profile of v2, /device:TPU:1, one launch (start us, length us, event | category | flops | bytes accessed | tf_op | source)
XLA Modules:
  0.0 63.4 jit_solution(4967018582115566384)
XLA Ops:
  0.6 0.0 copy-start
  0.6 0.0 copy-start.2
  0.7 7.4 %clade.1 = f32[512,128]{1,0:T(8,128)} custom-call(s32[2,31]{1,0:T(2,128)} %bitcast.30, f32[64,62]{1,0:T(8,128)} %bitcast.29, s32[1024,128]{1,0:T(8,128)} %bitcast.27), custom_call_target="tpu_custom_call" | custom-call | tf_op jit(solution)/shard_map/clade/pallas_call | solution.py:213
  8.0 10.2 %all-to-all-start = ((f32[16,32,128]{2,1,0:T(8,128)}), f32[16,32,128]{2,1,0:T(8,128)S(1)}, u32[]{:S(2)}, u32[]{:S(2)}) async-start(f32[16,32,128]{2,1,0:T(8,128)} %bitcast.26), calls=%async_computation | async-start | bytes 524288 | tf_op jit(solution)/shard_map/all_to_all | solution.py:233
  18.2 0.0 copy-start.1
  18.2 0.8 %copy-done.1 = f32[30,4,4,4]{0,3,2,1:T(4,128)S(1)} copy-done((f32[30,4,4,4]{0,3,2,1:T(4,128)S(1)}, f32[30,4,4,4]{0,3,2,1:T(4,128)}, u32[]{:S(2)}) %copy-start.1) | copy-done | bytes 7704
  19.0 0.9 %spread.1.refs_2_ = f32[480,8,128]{2,1,0:T(8,128)S(1)} custom-call(f32[64,30]{1,0:T(8,128)S(1)} %bitcast.23), custom_call_target="tpu_custom_call" | custom-call | flops 4194304 | bytes 2097152 | tf_op jit(solution)/shard_map/spread/pallas_call | solution.py:237
  19.9 0.0 copy-done
  19.9 0.1 dynamic-slice_bitcast_fusion.refs_3_
  20.0 10.0 %all-to-all-done = f32[16,32,128]{2,1,0:T(8,128)S(1)} async-done(((f32[16,32,128]{2,1,0:T(8,128)}), f32[16,32,128]{2,1,0:T(8,128)S(1)}, u32[]{:S(2)}, u32[]{:S(2)}) %all-to-all-start) | async-done | bytes 262176 | tf_op jit(solution)/shard_map/all_to_all | solution.py:233
  30.0 0.0 copy-done.2
  30.0 1.6 %upper.1 = (f32[2,128]{1,0:T(2,128)}, f32[16,128]{1,0:T(8,128)S(1)}) custom-call(s32[2,15]{1,0:T(2,128)S(1)} %bitcast.25, f32[512,128]{1,0:T(8,128)S(1)} %bitcast.22, f32[480,8,128]{2,1,0:T(8,128)S(1)} %spread.1.refs_2_, s32[2,128]{1,0:T(2,128)S(1)} %dynamic-slice_bitcast_fusion.refs_3_), custom_call_target="tpu_custom_call" | custom-call | tf_op jit(solution)/shard_map/upper/pallas_call | solution.py:247
  31.6 9.7 %all_to_all.15 = f32[16,1,128]{2,1,0:T(1,128)S(1)} all-to-all(f32[16,1,128]{2,1,0:T(1,128)S(1)} %bitcast.24), channel_id=1, replica_groups=mesh['site_0'=4,'site_1'=8,'clade_0'=8,'clade_1'=2] {'clade_0','clade_1'}, dimensions={0} | all-to-all | bytes 16384 | tf_op jit(solution)/shard_map/all_to_all | solution.py:194
  41.3 19.7 %all_to_all.16 = f32[32,1,128]{2,1,0:T(1,128)S(1)} all-to-all(f32[32,1,128]{2,1,0:T(1,128)S(1)} %broadcast_in_dim.2), channel_id=1, replica_groups=mesh['site_0'=4,'site_1'=8,'clade_0'=8,'clade_1'=2] {'site_0','site_1'}, dimensions={0} | all-to-all | bytes 32768 | tf_op jit(solution)/shard_map/all_to_all | solution.py:194
  61.1 0.6 reduce_sum.20
  (2 shorter events, 0.0 us)
Async XLA Ops:
  0.6 19.3 %copy-start = (s32[4096]{0:T(1024)S(1)}, s32[4096]{0:T(1024)}, u32[]{:S(2)}) copy-start(s32[4096]{0:T(1024)} %param.11) | copy-start | bytes 49156
  0.6 29.3 %copy-start.2 = (s32[15,2]{0,1:T(2,128)S(1)}, s32[15,2]{0,1:T(2,128)}, u32[]{:S(2)}) copy-start(s32[15,2]{0,1:T(2,128)} %param.10) | copy-start | bytes 364
  8.0 21.9 %all-to-all-start = ((f32[16,32,128]{2,1,0:T(8,128)}), f32[16,32,128]{2,1,0:T(8,128)S(1)}, u32[]{:S(2)}, u32[]{:S(2)}) async-start(f32[16,32,128]{2,1,0:T(8,128)} %bitcast.26), calls=%async_computation | async-start | bytes 524288 | tf_op jit(solution)/shard_map/all_to_all | solution.py:233
  18.2 0.8 %copy-start.1 = (f32[30,4,4,4]{0,3,2,1:T(4,128)S(1)}, f32[30,4,4,4]{0,3,2,1:T(4,128)}, u32[]{:S(2)}) copy-start(f32[30,4,4,4]{0,3,2,1:T(4,128)} %param.9) | copy-start | bytes 23044

commit v3 on v2

--- a/solution.py
+++ b/solution.py
@@ -6,9 +6,19 @@
 from jax.sharding import Mesh
 from jax.sharding import PartitionSpec as P
 
-CLADE = ("clade_0", "clade_1")
-SITE = ("site_0", "site_1")
-SITE_CLADE = SITE + CLADE
+CLADE = "clade"
+SITE = "site"
+SITE_CLADE = (SITE, CLADE)
+CLADE_FIRST = 8
+SITE_FIRST = 20
+
+
+def all_to_all(blocks, axis, first):
+    members = lax.axis_size(axis)
+    group = [(first + i) % members for i in range(members)]
+    return lax.all_to_all(
+        blocks, axis, split_axis=0, concat_axis=0, axis_index_groups=[group], tiled=True
+    )
 
 
 def splat(column_block, k):
@@ -26,7 +36,7 @@
 
 def clade_kernel(
     merges_hbm, rows_hbm, tips_hbm, out_hbm,
-    merges_ref, probs_ref, rows_ref, tips_ref, tables_ref, parts_ref, inv_ref, log_ref, root_ref, sems,
+    merges_ref, order_ref, probs_ref, rows_ref, tips_ref, tables_ref, parts_ref, top_ref, log_ref, root_ref, sems,
 ):
     copies = [
         pltpu.make_async_copy(source, target, sems.at[i])
@@ -42,6 +52,7 @@
     tiles = range(2 * groups // 8)
     log_ref[...] = jnp.zeros_like(log_ref)
     copies[0].wait()
+    copies[1].wait()
     blocks = []
     for k in range(16):
         rows = [rows_ref[4 * k + b : 4 * k + b + 1, :] for b in range(4)]
@@ -49,8 +60,14 @@
     for taxon in range(leaves):
         for k in range(16):
             tables_ref[taxon * 16 + k] = splat(blocks[k], taxon)
-    for copy in copies[1:]:
-        copy.wait()
+    pairs, others = jnp.int32(0), jnp.int32(0)
+    for j in range(merges):
+        is_pair = jnp.maximum(merges_ref[0, j], merges_ref[1, j]) < leaves
+        order_ref[0, pairs] = j
+        order_ref[1, others] = j
+        pairs = pairs + jnp.where(is_pair, 1, 0)
+        others = others + jnp.where(is_pair, 0, 1)
+    copies[3].wait()
 
     def codes(taxon):
         start = (taxon // 8) * (16 * groups) + taxon % 8
@@ -70,9 +87,16 @@
 
         return planes
 
+    def add_logs(invs):
+        for t in tiles:
+            rows = slice(8 * t, 8 * t + 8)
+            log_ref[rows, :] = log_ref[rows, :] - sum(jnp.log(inv[t]) for inv in invs)
+
     def inner_branch(node):
         inner = node - leaves
-        inv = [inv_ref[inner, 8 * t : 8 * t + 8, :] for t in tiles]
+        inv = [
+            pl.reciprocal(top_ref[inner, 8 * t : 8 * t + 8, :], approx=True) for t in tiles
+        ]
 
         def planes(rate):
             part = [
@@ -90,9 +114,13 @@
                     for t in tiles
                 ]
 
+        planes.inv = inv
         return planes
 
     def merge(j, one, other):
+        add_logs_of = [branch.inv for branch in (one, other) if hasattr(branch, "inv")]
+        if add_logs_of:
+            add_logs(add_logs_of)
         biggest = None
         for rate in range(4):
             firsts = list(one(rate))
@@ -102,35 +130,41 @@
                     parts_ref[j * 16 + rate * 4 + state, 8 * t : 8 * t + 8, :] = q[t]
                 biggest = q if biggest is None else [jnp.maximum(biggest[t], q[t]) for t in tiles]
         for t in tiles:
-            rows = slice(8 * t, 8 * t + 8)
-            inv = pl.reciprocal(biggest[t], approx=True)
-            inv_ref[j, rows, :] = inv
-            log_ref[rows, :] = log_ref[rows, :] - jnp.log(inv)
-
-    def step(j, _):
+            top_ref[j, 8 * t : 8 * t + 8, :] = biggest[t]
+
+    def two_pairs(i, _):
+        for place in (2 * i, jnp.minimum(2 * i + 1, pairs - 1)):
+            j = order_ref[0, place]
+            merge(j, leaf_branch(merges_ref[0, j]), leaf_branch(merges_ref[1, j]))
+        return 0
+
+    def step(i, _):
+        j = order_ref[1, i]
         c, d = merges_ref[0, j], merges_ref[1, j]
+        high, low = jnp.maximum(c, d), jnp.minimum(c, d)
         leaf, inner = leaf_branch, inner_branch
-        high, low = jnp.maximum(c, d), jnp.minimum(c, d)
-        pl.when(high < leaves)(lambda: merge(j, leaf(high), leaf(low)))
-        pl.when((high >= leaves) & (low < leaves))(lambda: merge(j, inner(high), leaf(low)))
+        pl.when(low < leaves)(lambda: merge(j, inner(high), leaf(low)))
         pl.when(low >= leaves)(lambda: merge(j, inner(high), inner(low)))
         return 0
 
-    lax.fori_loop(0, merges, step, 0)
+    lax.fori_loop(0, (pairs + 1) // 2, two_pairs, 0)
+    copies[2].wait()
+    lax.fori_loop(0, others, step, 0)
 
     last = merges - 1
     half = 8 * 32
     sends = []
     for part in range(groups // 8):
+        place = (part - CLADE_FIRST // 8) % (groups // 8)
         for h in range(2):
             rows = slice(h * groups + 8 * part, h * groups + 8 * part + 8)
-            scale = log_ref[rows, :] + jnp.log(inv_ref[last, rows, :])
+            scale = log_ref[rows, :]
             for rate in range(4):
                 for state in range(4):
                     value = jnp.log(parts_ref[last * 16 + rate * 4 + state, rows, :]) + scale
-                    start = part * half + state * 8 + rate * 2 + h
+                    start = place * half + state * 8 + rate * 2 + h
                     root_ref[pl.ds(start, 8, stride=32), :] = value
-        span = pl.ds(part * half, half)
+        span = pl.ds(place * half, half)
         sends.append(pltpu.make_async_copy(root_ref.at[span], out_hbm.at[span], sems.at[4 + part]))
         sends[-1].start()
     for send in sends:
@@ -155,7 +189,8 @@
 
     scale = jnp.zeros((8, 128), jnp.float32)
     for k in range(clades):
-        rows = [roots_ref[k * 32 + 8 * a : k * 32 + 8 * a + 8, :] for a in range(4)]
+        start = (k - CLADE_FIRST) % clades * 32
+        rows = [roots_ref[start + 8 * a : start + 8 * a + 8, :] for a in range(4)]
         top = jnp.maximum(jnp.maximum(rows[0], rows[1]), jnp.maximum(rows[2], rows[3]))
         top = over_rates(jnp.maximum, top)
         scale = scale + top
@@ -190,8 +225,8 @@
     sum_ref[...] = jnp.broadcast_to(weighted[0:1, :] + weighted[1:2, :], sum_ref.shape)
 
 
-def sum_over(rows, axes, copies):
-    got = lax.all_to_all(rows, axes, split_axis=0, concat_axis=0, tiled=True)
+def sum_over(rows, axis, first, copies):
+    got = all_to_all(rows, axis, first)
     return jnp.broadcast_to(jnp.sum(got, axis=0, keepdims=True), (copies,) + got.shape[1:])
 
 
@@ -217,6 +252,7 @@
         out_specs=hbm,
         scratch_shapes=[
             pltpu.SMEM(merges.shape, jnp.int32),
+            pltpu.SMEM((2, leaves), jnp.int32),
             pltpu.SMEM(rows.shape, jnp.float32),
             pltpu.VMEM(rows.shape, jnp.float32),
             pltpu.VMEM(tiled.shape, jnp.int32),
@@ -230,9 +266,7 @@
         name="clade",
     )(merges, rows, tiled)
 
-    got = lax.all_to_all(
-        logs.reshape(clades, 32, 128), CLADE, split_axis=0, concat_axis=0, tiled=True
-    )
+    got = all_to_all(logs.reshape(clades, 32, 128), CLADE, CLADE_FIRST)
     upper_rows = upper_transition.transpose(1, 2, 3, 0).reshape(64, -1)
     spread = pl.pallas_call(
         spread_kernel,
@@ -257,13 +291,13 @@
         name="upper",
     )(upper_children.T, got.reshape(clades * 32, 128), spread, own.reshape(piece // 128, 128))
 
-    part = sum_over(addend.reshape(clades, 1, 128), CLADE, groups)
-    whole = sum_over(part, SITE, 1)
+    part = sum_over(addend.reshape(clades, 1, 128), CLADE, CLADE_FIRST, groups)
+    whole = sum_over(part, SITE, SITE_FIRST, 1)
     return weighted.reshape(piece), jnp.sum(whole) / (sites * groups)
 
 
 def solution(mesh):
-    torus = Mesh(mesh.devices.reshape(4, 8, 8, 2), SITE_CLADE)
+    torus = Mesh(mesh.devices.reshape(32, 16), SITE_CLADE)
     return jax.shard_map(
         per_device,
         mesh=torus,

time: 63.8 us -> 56.9 us (0.89)
  blocking collectives: 29.4 us -> 23.3 us
  waiting for transfers between devices: 10 us -> 5.59 us
  starting transfers between devices: 10.2 us -> 13.8 us
    all_to_all x2, blocking collectives: 29.4 us -> 23.3 us  [all_to_all(): lax.all_to_all(blocks, axis, split_axis=0, concat_axis=0, axis_index_grou...]
    all_to_all x1, waiting for transfers between devices: 10 us -> 5.59 us  [all_to_all(): lax.all_to_all(blocks, axis, split_axis=0, concat_axis=0, axis_index_grou...]
    all_to_all x1, starting transfers between devices: 10.2 us -> 13.8 us  [all_to_all(): lax.all_to_all(blocks, axis, split_axis=0, concat_axis=0, axis_index_grou...]
  transfers between devices with their start and end apart: 1 -> 1, of which waited for: 1 -> 1; matrix products, arithmetic and copies ran while one was open for 0% -> 0% of each run, Pallas kernels for 1% -> 2%
where the time goes in v3:
time: 56.9 us; the launch traced here: 56 us
  blocking collectives  23.3 us (41%)
  starting transfers between devices  13.8 us (24%)
  Pallas kernels  9.48 us (17%)
  waiting for transfers between devices  5.59 us (10%)
  between operations  2.44 us (4%)
  local copies, waits for them, and re-layouts  0.86 us (2%)
  other arithmetic  0.64 us (1%)
    all_to_all x2, blocking collectives, all_to_all(): lax.all_to_all(blocks, axis, split_axis=0, concat_axis=0, axis_index_grou...  23.3 us
    all_to_all x1, starting transfers between devices, all_to_all(): lax.all_to_all(blocks, axis, split_axis=0, concat_axis=0, axis_index_grou...  13.8 us
    pallas_call x1, Pallas kernels, per_device(): pl.pallas_call(clade_kernel, out_shape=jax.ShapeDtypeStruct((clades * 32,...  6.96 us
    all_to_all x1, waiting for transfers between devices, all_to_all(): lax.all_to_all(blocks, axis, split_axis=0, concat_axis=0, axis_index_grou...  5.59 us
    pallas_call x1, Pallas kernels, per_device(): pl.pallas_call(lambda *refs: upper_kernel(float(leaves * clades), *refs),...  1.61 us
  transfers between devices with their start and end apart: 1, of which 1 were waited for; matrix products, arithmetic and copies ran while one was open for 0% of the time, Pallas kernels for 2%

profile of v3, /device:TPU:1, one launch (start us, length us, event | category | flops | bytes accessed | tf_op | source)
XLA Modules:
  0.0 56.0 jit_solution(11391467078190235938)
XLA Ops:
  0.6 0.0 copy-start
  0.6 0.0 copy-start.2
  0.7 7.0 %clade.1 = f32[512,128]{1,0:T(8,128)} custom-call(s32[2,31]{1,0:T(2,128)} %bitcast.30, f32[64,62]{1,0:T(8,128)} %bitcast.29, s32[1024,128]{1,0:T(8,128)} %bitcast.27), custom_call_target="tpu_custom_call" | custom-call | tf_op jit(solution)/shard_map/clade/pallas_call | solution.py:248
  7.6 13.8 %all-to-all-start = ((f32[16,32,128]{2,1,0:T(8,128)}), f32[16,32,128]{2,1,0:T(8,128)S(1)}, u32[]{:S(2)}, u32[]{:S(2)}) async-start(f32[16,32,128]{2,1,0:T(8,128)} %bitcast.26), calls=%async_computation | async-start | bytes 524288 | tf_op jit(solution)/shard_map/all_to_all | solution.py:19
  21.4 0.0 copy-start.1
  21.4 0.8 %copy-done.1 = f32[30,4,4,4]{0,3,2,1:T(4,128)S(1)} copy-done((f32[30,4,4,4]{0,3,2,1:T(4,128)S(1)}, f32[30,4,4,4]{0,3,2,1:T(4,128)}, u32[]{:S(2)}) %copy-start.1) | copy-done | bytes 7704
  22.1 0.9 %spread.1.refs_2_ = f32[480,8,128]{2,1,0:T(8,128)S(1)} custom-call(f32[64,30]{1,0:T(8,128)S(1)} %bitcast.23), custom_call_target="tpu_custom_call" | custom-call | flops 4194304 | bytes 2097152 | tf_op jit(solution)/shard_map/spread/pallas_call | solution.py:271
  23.1 0.0 copy-done
  23.1 0.1 dynamic-slice_bitcast_fusion.refs_3_
  23.1 5.6 %all-to-all-done = f32[16,32,128]{2,1,0:T(8,128)S(1)} async-done(((f32[16,32,128]{2,1,0:T(8,128)}), f32[16,32,128]{2,1,0:T(8,128)S(1)}, u32[]{:S(2)}, u32[]{:S(2)}) %all-to-all-start) | async-done | bytes 262176 | tf_op jit(solution)/shard_map/all_to_all | solution.py:19
  28.7 0.0 copy-done.2
  28.7 1.6 %upper.1 = (f32[2,128]{1,0:T(2,128)}, f32[16,128]{1,0:T(8,128)S(1)}) custom-call(s32[2,15]{1,0:T(2,128)S(1)} %bitcast.25, f32[512,128]{1,0:T(8,128)S(1)} %bitcast.22, f32[480,8,128]{2,1,0:T(8,128)S(1)} %spread.1.refs_2_, s32[2,128]{1,0:T(2,128)S(1)} %dynamic-slice_bitcast_fusion.refs_3_), custom_call_target="tpu_custom_call" | custom-call | tf_op jit(solution)/shard_map/upper/pallas_call | solution.py:281
  30.3 9.1 %all_to_all.15 = f32[16,1,128]{2,1,0:T(1,128)S(1)} all-to-all(f32[16,1,128]{2,1,0:T(1,128)S(1)} %bitcast.24), channel_id=1, replica_groups={{8,9,10,11,12,13,14,15,0,1,2,3,4,5,6,7},{24,25,26,27,28,29,30,31,16,17,..., dimensions={0} | all-to-all | bytes 16384 | tf_op jit(solution)/shard_map/all_to_all | solution.py:19
  39.5 14.2 %all_to_all.16 = f32[32,1,128]{2,1,0:T(1,128)S(1)} all-to-all(f32[32,1,128]{2,1,0:T(1,128)S(1)} %broadcast_in_dim.2), channel_id=1, replica_groups={{320,336,352,368,384,400,416,432,448,464,480,496,0,16,32,48,64,80,96,11..., dimensions={0} | all-to-all | bytes 32768 | tf_op jit(solution)/shard_map/all_to_all | solution.py:19
  53.7 0.6 %reduce_sum.20 = f32[]{:T(128)} reduce(f32[32,1,128]{2,0,1:T(8,128)S(1)} %bitcast.28, f32[]{:T(128)} %constant.5.clone.1), dimensions={0,1,2}, to_apply=%region_1.0 | reduce | flops 4095 | bytes 16392 | tf_op jit(solution)/shard_map/reduce_sum | solution.py:296
  (2 shorter events, 0.0 us)
Async XLA Ops:
  0.6 22.4 %copy-start = (s32[4096]{0:T(1024)S(1)}, s32[4096]{0:T(1024)}, u32[]{:S(2)}) copy-start(s32[4096]{0:T(1024)} %param.11) | copy-start | bytes 49156
  0.6 28.1 %copy-start.2 = (s32[15,2]{0,1:T(2,128)S(1)}, s32[15,2]{0,1:T(2,128)}, u32[]{:S(2)}) copy-start(s32[15,2]{0,1:T(2,128)} %param.10) | copy-start | bytes 364
  7.6 21.1 %all-to-all-start = ((f32[16,32,128]{2,1,0:T(8,128)}), f32[16,32,128]{2,1,0:T(8,128)S(1)}, u32[]{:S(2)}, u32[]{:S(2)}) async-start(f32[16,32,128]{2,1,0:T(8,128)} %bitcast.26), calls=%async_computation | async-start | bytes 524288 | tf_op jit(solution)/shard_map/all_to_all | solution.py:19
  21.4 0.8 %copy-start.1 = (f32[30,4,4,4]{0,3,2,1:T(4,128)S(1)}, f32[30,4,4,4]{0,3,2,1:T(4,128)}, u32[]{:S(2)}) copy-start(f32[30,4,4,4]{0,3,2,1:T(4,128)} %param.9) | copy-start | bytes 23044

commit v4 on v3

--- a/solution.py
+++ b/solution.py
@@ -9,8 +9,9 @@
 CLADE = "clade"
 SITE = "site"
 SITE_CLADE = (SITE, CLADE)
-CLADE_FIRST = 8
-SITE_FIRST = 20
+CLADE_FIRST = 9
+SUM_FIRST = 9
+SITE_FIRST = 21
 
 
 def all_to_all(blocks, axis, first):
@@ -152,21 +153,25 @@
     lax.fori_loop(0, others, step, 0)
 
     last = merges - 1
-    half = 8 * 32
+    runs = [(0, CLADE_FIRST, groups - CLADE_FIRST), (CLADE_FIRST, groups, 0)]
     sends = []
     for part in range(groups // 8):
-        place = (part - CLADE_FIRST // 8) % (groups // 8)
         for h in range(2):
             rows = slice(h * groups + 8 * part, h * groups + 8 * part + 8)
             scale = log_ref[rows, :]
             for rate in range(4):
                 for state in range(4):
                     value = jnp.log(parts_ref[last * 16 + rate * 4 + state, rows, :]) + scale
-                    start = place * half + state * 8 + rate * 2 + h
+                    start = part * 256 + state * 8 + rate * 2 + h
                     root_ref[pl.ds(start, 8, stride=32), :] = value
-        span = pl.ds(place * half, half)
-        sends.append(pltpu.make_async_copy(root_ref.at[span], out_hbm.at[span], sems.at[4 + part]))
-        sends[-1].start()
+        while len(sends) < 2 and runs[len(sends)][1] <= 8 * part + 8:
+            low, high, place = runs[len(sends)]
+            span = pl.ds(low * 32, (high - low) * 32)
+            target = pl.ds(place * 32, (high - low) * 32)
+            sends.append(
+                pltpu.make_async_copy(root_ref.at[span], out_hbm.at[target], sems.at[4 + len(sends)])
+            )
+            sends[-1].start()
     for send in sends:
         send.wait()
 
@@ -223,6 +228,12 @@
     weighted = weights_ref[...].astype(jnp.float32) * loglik * (1.0 / total_taxa)
     out_ref[...] = weighted
     sum_ref[...] = jnp.broadcast_to(weighted[0:1, :] + weighted[1:2, :], sum_ref.shape)
+
+
+def finish_kernel(total_sites, parts_ref, weighted_ref, out_ref, mean_ref):
+    out_ref[...] = weighted_ref[...]
+    by_lane = jnp.sum(parts_ref[...], axis=0, keepdims=True)
+    mean_ref[...] = jnp.sum(by_lane, axis=1, keepdims=True) * (1.0 / total_sites)
 
 
 def sum_over(rows, axis, first, copies):
@@ -291,9 +302,20 @@
         name="upper",
     )(upper_children.T, got.reshape(clades * 32, 128), spread, own.reshape(piece // 128, 128))
 
-    part = sum_over(addend.reshape(clades, 1, 128), CLADE, CLADE_FIRST, groups)
-    whole = sum_over(part, SITE, SITE_FIRST, 1)
-    return weighted.reshape(piece), jnp.sum(whole) / (sites * groups)
+    part = sum_over(addend.reshape(clades, 1, 128), CLADE, SUM_FIRST, groups)
+    whole = all_to_all(part, SITE, SITE_FIRST).reshape(groups, 128)
+    weighted, mean = pl.pallas_call(
+        lambda *refs: finish_kernel(float(sites * groups), *refs),
+        out_shape=[
+            jax.ShapeDtypeStruct(weighted.shape, jnp.float32),
+            jax.ShapeDtypeStruct((1, 1), jnp.float32),
+        ],
+        in_specs=[vmem, vmem],
+        out_specs=[vmem, vmem],
+        compiler_params=pltpu.CompilerParams(vmem_limit_bytes=4 << 20),
+        name="finish",
+    )(whole, weighted)
+    return weighted.reshape(piece), mean.reshape(())
 
 
 def solution(mesh):

time: 56.9 us -> 53.9 us (0.947)
  between operations: 2.44 us -> 0.67 us
  other arithmetic: 0.64 us -> 0.03 us
    reduce_sum x1 -> x0, other arithmetic: 0.6 us -> none  [per_device(): return (weighted.reshape(piece), jnp.sum(whole) / (sites * groups))]
    pallas_call x0 -> x1, Pallas kernels: none -> 0.6 us  [per_device(): pl.pallas_call(lambda *refs: finish_kernel(float(sites * groups), *refs),...]
    pallas_call x1, Pallas kernels: 1.61 us -> 1.04 us  [per_device(): pl.pallas_call(lambda *refs: upper_kernel(float(leaves * clades), *refs),...]
where the time goes in v4:
time: 53.9 us; the launch traced here: 53 us
  blocking collectives  22.9 us (42%)
  starting transfers between devices  13.4 us (25%)
  Pallas kernels  9.6 us (18%)
  waiting for transfers between devices  5.6 us (10%)
  local copies, waits for them, and re-layouts  0.86 us (2%)
  between operations  0.67 us (1%)
    all_to_all x2, blocking collectives, all_to_all(): lax.all_to_all(blocks, axis, split_axis=0, concat_axis=0, axis_index_grou...  22.9 us
    all_to_all x1, starting transfers between devices, all_to_all(): lax.all_to_all(blocks, axis, split_axis=0, concat_axis=0, axis_index_grou...  13.4 us
    pallas_call x1, Pallas kernels, per_device(): pl.pallas_call(clade_kernel, out_shape=jax.ShapeDtypeStruct((clades * 32,...  7.06 us
    all_to_all x1, waiting for transfers between devices, all_to_all(): lax.all_to_all(blocks, axis, split_axis=0, concat_axis=0, axis_index_grou...  5.6 us
  transfers between devices with their start and end apart: 1, of which 1 were waited for; matrix products, arithmetic and copies ran while one was open for 0% of the time, Pallas kernels for 2%

profile of v4, /device:TPU:1, one launch (start us, length us, event | category | flops | bytes accessed | tf_op | source)
XLA Modules:
  0.0 53.0 jit_solution(1738748376898363931)
XLA Ops:
  0.6 0.0 copy-start
  0.6 0.0 copy-start.2
  0.7 7.1 %clade.1 = f32[512,128]{1,0:T(8,128)} custom-call(s32[2,31]{1,0:T(2,128)} %bitcast.31, f32[64,62]{1,0:T(8,128)} %bitcast.30, s32[1024,128]{1,0:T(8,128)} %bitcast.29), custom_call_target="tpu_custom_call" | custom-call | tf_op jit(solution)/shard_map/clade/pallas_call | solution.py:259
  7.7 13.4 %all-to-all-start = ((f32[16,32,128]{2,1,0:T(8,128)}), f32[16,32,128]{2,1,0:T(8,128)S(1)}, u32[]{:S(2)}, u32[]{:S(2)}) async-start(f32[16,32,128]{2,1,0:T(8,128)} %bitcast.28), calls=%async_computation | async-start | bytes 524288 | tf_op jit(solution)/shard_map/all_to_all | solution.py:20
  21.1 0.0 copy-start.1
  21.1 0.8 %copy-done.1 = f32[30,4,4,4]{0,3,2,1:T(4,128)S(1)} copy-done((f32[30,4,4,4]{0,3,2,1:T(4,128)S(1)}, f32[30,4,4,4]{0,3,2,1:T(4,128)}, u32[]{:S(2)}) %copy-start.1) | copy-done | bytes 7704
  21.9 0.9 %spread.1.refs_2_ = f32[480,8,128]{2,1,0:T(8,128)S(1)} custom-call(f32[64,30]{1,0:T(8,128)S(1)} %bitcast.25), custom_call_target="tpu_custom_call" | custom-call | flops 4194304 | bytes 2097152 | tf_op jit(solution)/shard_map/spread/pallas_call | solution.py:282
  22.8 0.0 copy-done
  22.8 0.1 dynamic-slice_bitcast_fusion.refs_3_
  22.9 5.6 %all-to-all-done = f32[16,32,128]{2,1,0:T(8,128)S(1)} async-done(((f32[16,32,128]{2,1,0:T(8,128)}), f32[16,32,128]{2,1,0:T(8,128)S(1)}, u32[]{:S(2)}, u32[]{:S(2)}) %all-to-all-start) | async-done | bytes 262176 | tf_op jit(solution)/shard_map/all_to_all | solution.py:20
  28.5 0.0 copy-done.2
  28.5 1.0 %upper.1 = (f32[2,128]{1,0:T(2,128)S(1)}, f32[16,128]{1,0:T(8,128)S(1)}) custom-call(s32[2,15]{1,0:T(2,128)S(1)} %bitcast.27, f32[512,128]{1,0:T(8,128)S(1)} %bitcast.23, f32[480,8,128]{2,1,0:T(8,128)S(1)} %spread.1.refs_2_, s32[2,128]{1,0:T(2,128)S(1)} %dynamic-slice_bitcast_fusion.refs_3_), custom_call_target="tpu_custom_call" | custom-call | tf_op jit(solution)/shard_map/upper/pallas_call | solution.py:292
  29.5 9.1 %all_to_all.15 = f32[16,1,128]{2,1,0:T(1,128)S(1)} all-to-all(f32[16,1,128]{2,1,0:T(1,128)S(1)} %bitcast.26), channel_id=1, replica_groups={{9,10,11,12,13,14,15,0,1,2,3,4,5,6,7,8},{25,26,27,28,29,30,31,16,17,18,..., dimensions={0} | all-to-all | bytes 16384 | tf_op jit(solution)/shard_map/all_to_all | solution.py:20
  38.6 13.8 %all_to_all.16 = f32[32,1,128]{2,1,0:T(1,128)S(1)} all-to-all(f32[32,1,128]{2,1,0:T(1,128)S(1)} %broadcast_in_dim.2), channel_id=1, replica_groups={{336,352,368,384,400,416,432,448,464,480,496,0,16,32,48,64,80,96,112,12..., dimensions={0} | all-to-all | bytes 32768 | tf_op jit(solution)/shard_map/all_to_all | solution.py:20
  52.4 0.6 %finish.1 = (f32[2,128]{1,0:T(2,128)}, f32[1,1]{1,0:T(1,128)}) custom-call(f32[32,128]{1,0:T(8,128)S(1)} %bitcast.24, f32[2,128]{1,0:T(2,128)S(1)} %get-tuple-element.7.refs_1_), custom_call_target="tpu_custom_call" | custom-call | tf_op jit(solution)/shard_map/finish/pallas_call | solution.py:307
  (2 shorter events, 0.0 us)
Async XLA Ops:
  0.6 22.2 %copy-start = (s32[4096]{0:T(1024)S(1)}, s32[4096]{0:T(1024)}, u32[]{:S(2)}) copy-start(s32[4096]{0:T(1024)} %param.11) | copy-start | bytes 49156
  0.6 27.8 %copy-start.2 = (s32[15,2]{0,1:T(2,128)S(1)}, s32[15,2]{0,1:T(2,128)}, u32[]{:S(2)}) copy-start(s32[15,2]{0,1:T(2,128)} %param.10) | copy-start | bytes 364
  7.7 20.7 %all-to-all-start = ((f32[16,32,128]{2,1,0:T(8,128)}), f32[16,32,128]{2,1,0:T(8,128)S(1)}, u32[]{:S(2)}, u32[]{:S(2)}) async-start(f32[16,32,128]{2,1,0:T(8,128)} %bitcast.28), calls=%async_computation | async-start | bytes 524288 | tf_op jit(solution)/shard_map/all_to_all | solution.py:20
  21.1 0.8 %copy-start.1 = (f32[30,4,4,4]{0,3,2,1:T(4,128)S(1)}, f32[30,4,4,4]{0,3,2,1:T(4,128)}, u32[]{:S(2)}) copy-start(f32[30,4,4,4]{0,3,2,1:T(4,128)} %param.9) | copy-start | bytes 23044
